TPU v7x, 32 devices: a whole 2x2x4 slice. The times are simulated.
32 devices in a mesh: blk: 32 (over z, y, x, core).
Axes of the slice: x: 2, y: 2, z: 4, core: 2. Of those that a mesh axis runs over, the one named last changes fastest.
Arguments:
- tiles: float32 [128, 3, 256, 256], P('blk'), may hold values from -0.109375 to 0.109375
- offsets: int32 [128, 3], P('blk'), may hold values from -2 to 2, as said below
- start: float32 [32768, 128], P('blk'), may hold values from -6 to 6
Outputs:
- grams: float32 [2, 8, 8, 128], replicated
- final: float32 [32768, 128], P('blk')
Inputs may be any that keep to these rules, and one draw needn't show every extreme that they name: The 3 offsets of a block row are all different.
All inputs are finite; a program needn't handle non-finite values.
Results may differ from a plain program's by a relative error of at most 0.00018.
Values sent between devices are 32-bit elements; how exact they have to be, the bound alone decides.
A program may use at most 128 MiB of HBM per device.

v0:
```python
import functools

import jax
import jax.numpy as jnp
from jax import lax
from jax.experimental import pallas as pl
from jax.experimental.pallas import tpu as pltpu
from jax.sharding import PartitionSpec as P

REACH = 2
OUTER = 2
DEPTH = 4
SPLIT = 2
MESH = pl.DeviceIdType.MESH
F32 = jnp.float32
BF16 = jnp.bfloat16


def halves(x):
    high = x.astype(BF16)
    return high, (x - high.astype(F32)).astype(BF16)


def kernel(
    n,
    levels,
    total_rows,
    off_ref,
    tiles_hbm,
    start_hbm,
    gram_ref,
    final_ref,
    raw,
    fwd,
    adj,
    basis,
    field,
    image,
    parts,
    halo,
    give,
    got,
    gram,
    sums,
    heard,
    load_sem,
    send_sem,
    recv_sem,
    sum_send,
    sum_recv,
):
    nblk, slots, tile, _ = raw.shape
    probes = basis.shape[3]
    me = lax.axis_index("blk")
    slow = lax.rem(me, 2)
    fast = 1 - slow
    left, right = lax.rem(me + n - 1, n), lax.rem(me + 1, n)
    partners = []
    for b in range(levels):
        s = 1 << b
        partners.append(me + s * (1 - 2 * lax.rem(me // s, 2)))

    load_start = pltpu.make_async_copy(start_hbm, basis.at[0], load_sem.at[0])
    load_start.start()
    load_tiles = pltpu.make_async_copy(tiles_hbm, raw, load_sem.at[1])
    load_tiles.start()

    barrier = pltpu.get_barrier_semaphore()
    for other in [left, right] + partners:
        pl.semaphore_signal(barrier, inc=1, device_id=(other,), device_id_type=MESH)

    def block(side, k):
        return side * (nblk - 1) + k * (1 - 2 * side)

    def beyond(side, k):
        return side * (nblk + 1 + 2 * k) - 1 - k

    def remote(src, dst, here, there, side):
        return pltpu.make_async_remote_copy(
            src_ref=src,
            dst_ref=dst,
            send_sem=send_sem.at[here],
            recv_sem=recv_sem.at[there],
            device_id=(lax.rem(me + n - 1 + 2 * side, n),),
            device_id_type=MESH,
        )

    piece = tile // SPLIT

    def span(h):
        return pl.ds(h * piece, piece)

    def send_p(t, side, k, h):
        here, there = side * REACH + k, (1 - side) * REACH + k
        src, dst = basis.at[t, block(side, k), span(h)], halo.at[there, span(h)]
        remote(src, dst, here * SPLIT + h, there * SPLIT + h, side).start()

    def wait_p(t, side, k):
        here = side * REACH + k
        for h in range(SPLIT):
            src, dst = basis.at[t, block(side, k), span(h)], halo.at[here, span(h)]
            remote(src, dst, here * SPLIT + h, here * SPLIT + h, side).wait()

    more = 2 * REACH * SPLIT

    def send_part(side, k, h):
        here, there = side * REACH + k, (1 - side) * REACH + k
        src, dst = give.at[here, span(h)], got.at[there, span(h)]
        remote(src, dst, more + here * SPLIT + h, more + there * SPLIT + h, side).start()

    def wait_part(side, k, h):
        here = side * REACH + k
        sem = more + here * SPLIT + h
        remote(give.at[here, span(h)], got.at[here, span(h)], sem, sem, side).wait()

    def sum_step(outer, b):
        k = outer * levels + b
        return pltpu.make_async_remote_copy(
            src_ref=sums.at[outer * (levels + 1) + b],
            dst_ref=heard.at[k],
            send_sem=sum_send.at[k],
            recv_sem=sum_recv.at[k],
            device_id=(partners[b],),
            device_id_type=MESH,
        )

    def source(i, d):
        index = nblk * slots
        for k in range(slots):
            index = jnp.where(off_ref[i, k] == d, i * slots + k, index)
        return index

    gram[...] = jnp.zeros_like(gram)
    parts[nblk * slots] = jnp.zeros((tile, probes), F32)

    load_start.wait()
    pl.semaphore_wait(barrier, 2 + levels)
    for k in range(REACH):
        for h in range(SPLIT):
            send_p(0, slow, k, h)
            send_p(0, fast, k, h)
    load_tiles.wait()

    def prepare(i, carry):
        for k in range(slots):
            value = raw[i, k]
            high, low = halves(value)
            fwd[i, pl.ds(0, tile), pl.ds(k * tile, tile)] = high
            fwd[i, pl.ds(tile, tile), pl.ds(k * tile, tile)] = low
            high, low = halves(value.T)
            adj[i, pl.ds(2 * k * tile, tile), :] = high
            adj[i, pl.ds((2 * k + 1) * tile, tile), :] = low
        return carry

    lax.fori_loop(0, nblk, prepare, 0)

    def keep(ref, i, value):
        high, low = halves(value)
        ref[i, :, pl.ds(0, probes)] = high
        ref[i, :, pl.ds(probes, probes)] = low

    def joined(r, base):
        top = r[base : base + tile]
        low = r[base + tile : base + 2 * tile]
        return (top[:, :probes] + top[:, probes:]) + (low[:, :probes] + low[:, probes:])

    def gram_rows(t):
        def one(u, carry):
            prod = (basis[t] * basis[u]).reshape(-1, probes)
            s = jnp.sum(prod.reshape(-1, 8, probes), axis=0)
            gram[pl.ds(t * 2 * DEPTH + u, 1), :] = jnp.sum(s, axis=0, keepdims=True)
            return carry

        lax.fori_loop(0, t + 1, one, 0)

    def forward(t, i):
        rhs = jnp.concatenate([field[i + REACH + off_ref[i, k]] for k in range(slots)], axis=0)
        q = joined(jnp.dot(fwd[i], rhs, preferred_element_type=F32), 0)
        basis[t + 1, i] = q
        keep(image, i, q)
        r = jnp.dot(adj[i], image[i], preferred_element_type=F32)
        for k in range(slots):
            parts[i * slots + k] = joined(r, 2 * k * tile)

    def arrive(t, side, k):
        wait_p(t, side, k)
        keep(field, beyond(side, k) + REACH, halo[side * REACH + k])

    def hand_over(side):
        for k in range(REACH):
            for h in range(SPLIT):
                total = None
                for r in range(REACH - k):
                    index = source(block(side, r), (2 * side - 1) * (r + 1 + k))
                    term = parts[index, span(h)]
                    total = term if total is None else total + term
                give[side * REACH + k, span(h)] = total
                send_part(side, k, h)

    def gathered(target):
        total = None
        for i in range(nblk):
            if abs(target - i) <= REACH:
                term = parts[source(i, target - i)]
                total = term if total is None else total + term
        return total

    def take(t, side, k, last):
        for h in range(SPLIT):
            wait_part(side, k, h)
            basis[t, block(side, k), span(h)] += got[side * REACH + k, span(h)]
            if not last:
                send_p(t, side, k, h)

    def pair(outer, j, last):
        t = 2 * j
        for i in range(nblk):
            keep(field, i + REACH, basis[t, i])
        gram_rows(t)
        for k in range(REACH):
            arrive(t, fast, k)
        for i in range(REACH, nblk - REACH):
            forward(t, i)
        for k in reversed(range(REACH)):
            forward(t, block(fast, k))
        hand_over(fast)
        for k in range(REACH):
            arrive(t, slow, k)
            forward(t, block(slow, REACH - 1 - k))
        hand_over(slow)
        if last:
            gram_rows(t + 1)
            sums[outer * (levels + 1)] = gram[...]
            sum_step(outer, 0).start()
        for i in range(nblk):
            basis[t + 2, i] = gathered(i)
        for k in range(REACH):
            take(t + 2, fast, k, last)
        if last:
            for b in range(levels):
                sum_step(outer, b).wait()
                k = outer * (levels + 1) + b
                sums[k + 1] = sums[k] + heard[outer * levels + b]
                if b + 1 < levels:
                    sum_step(outer, b + 1).start()
        else:
            gram_rows(t + 1)
        for k in range(REACH):
            take(t + 2, slow, k, last)

    def outer_step(outer, carry):
        def inner(j, c):
            pair(outer, j, False)
            return c

        lax.fori_loop(0, DEPTH - 1, inner, 0)
        pair(outer, DEPTH - 1, True)
        total = outer * (levels + 1) + levels
        size = 2 * DEPTH
        corner = sums[total, pl.ds(size * size - 1, 1), :] / total_rows
        scale = 1.0 / jnp.sqrt(corner + 0.25)
        basis[0] = basis[size] * scale[None]

        @pl.when(outer < OUTER - 1)
        def _():
            for k in range(REACH):
                for h in range(SPLIT):
                    send_p(0, slow, k, h)
                    send_p(0, fast, k, h)

        when = [2 * a for a in range(DEPTH)] + [2 * a + 1 for a in range(DEPTH)]
        for a in range(size):
            for b in range(size):
                row = max(when[a], when[b]) * size + min(when[a], when[b])
                gram_ref[outer, pl.ds(a * size + b, 1), :] = (
                    sums[total, pl.ds(row, 1), :] / total_rows
                )
        return carry

    lax.fori_loop(0, OUTER, outer_step, 0)
    final_ref[...] = basis[0]


def on_device(tiles, offsets, start):
    n = lax.axis_size("blk")
    levels = n.bit_length() - 1
    assert n == 1 << levels
    nblk, slots, tile, _ = tiles.shape
    rows, probes = start.shape
    assert nblk >= 2 * REACH
    size = 2 * DEPTH
    dma = pltpu.SemaphoreType.DMA
    grams, final = pl.pallas_call(
        functools.partial(kernel, n, levels, float(rows * n)),
        out_shape=(
            jax.ShapeDtypeStruct((OUTER, size * size, probes), F32),
            jax.ShapeDtypeStruct((nblk, tile, probes), F32),
        ),
        in_specs=[
            pl.BlockSpec(memory_space=pltpu.SMEM),
            pl.BlockSpec(memory_space=pl.ANY),
            pl.BlockSpec(memory_space=pl.ANY),
        ],
        out_specs=(pl.BlockSpec(memory_space=pltpu.VMEM), pl.BlockSpec(memory_space=pltpu.VMEM)),
        scratch_shapes=[
            pltpu.VMEM(tiles.shape, F32),
            pltpu.VMEM((nblk, 2 * tile, slots * tile), BF16),
            pltpu.VMEM((nblk, 2 * slots * tile, tile), BF16),
            pltpu.VMEM((size + 1, nblk, tile, probes), F32),
            pltpu.VMEM((nblk + 2 * REACH, tile, 2 * probes), BF16),
            pltpu.VMEM((nblk, tile, 2 * probes), BF16),
            pltpu.VMEM((nblk * slots + 1, tile, probes), F32),
        ]
        + [pltpu.VMEM((2 * REACH, tile, probes), F32)] * 3
        + [
            pltpu.VMEM((size * size, probes), F32),
            pltpu.VMEM((OUTER * (levels + 1), size * size, probes), F32),
            pltpu.VMEM((OUTER * levels, size * size, probes), F32),
            dma((2,)),
            dma((4 * REACH * SPLIT,)),
            dma((4 * REACH * SPLIT,)),
            dma((OUTER * levels,)),
            dma((OUTER * levels,)),
        ],
        compiler_params=pltpu.CompilerParams(collective_id=0, has_side_effects=True),
    )(offsets, tiles, start.reshape(nblk, tile, probes))
    return grams.reshape(OUTER, size, size, probes), final.reshape(rows, probes)


def solution(mesh):
    placed = (P("blk", None, None, None), P("blk", None), P("blk", None))
    return jax.shard_map(
        on_device, mesh=mesh, in_specs=placed, out_specs=(P(), P("blk", None)), check_vma=False
    )
```

profile of v0, /device:TPU:0, one launch (start us, length us, event | category | flops | bytes accessed | tf_op | source)
XLA Modules:
  0.0 141.7 jit_solution(6489958903953648261)
XLA Ops:
  0.6 137.7 %shard_map.50 = (f32[2,64,128]{2,1,0:T(8,128)}, f32[4,256,128]{2,1,0:T(8,128)}) custom-call(s32[4,3]{1,0:T(4,128)} %off_ref.1, f32[4,3,256,256]{3,2,1,0:T(8,128)} %tiles_hbm.1, f32[4,256,128]{2,1,0:T(8,128)} %bitcast.3), custom_call_target="tpu_custom_call" | custom-call | tf_op jit(solution)/shard_map/pallas_call | solution.py:293
  138.4 1.5 %copy.7 = f32[2,8,8,128]{3,2,1,0:T(8,128)} copy(f32[2,8,8,128]{3,2,1,0:T(8,128)} %bitcast.5) | data formatting | bytes 131072
  139.8 1.9 %copy.8 = f32[1024,128]{1,0:T(8,128)} copy(f32[1024,128]{1,0:T(8,128)} %bitcast.4) | data formatting | bytes 1048576
where the time goes:
time: 142 us
  Pallas kernels  138 us (97%)
  local copies, waits for them, and re-layouts  3.34 us (2%)
    pallas_call x1, Pallas kernels, on_device(): pl.pallas_call(functools.partial(kernel, n, levels, float(rows * n)), out...  138 us
    unnamed x2, local copies, waits for them, and re-layouts  3.34 us

commit v1 on v0

v1 whole, which is shorter than its diff:
```python
import functools

import jax
import jax.numpy as jnp
from jax import lax
from jax.experimental import pallas as pl
from jax.experimental.pallas import tpu as pltpu
from jax.sharding import PartitionSpec as P

REACH = 2
OUTER = 2
DEPTH = 4
SIZE = 2 * DEPTH
STREAMS = 2
FIRST = [0, 1, 3, 5, 8, 11, 16, 20]
GROUPS = [(0, 8), (8, 8), (16, 16)]
CLOSES = [3, 5, 7]
GAUGE = 3
GROWTH = 2.0 ** (14 * (SIZE - 1 - GAUGE))
MESH = pl.DeviceIdType.MESH
F32 = jnp.float32
BF16 = jnp.bfloat16


def halves(x):
    high = x.astype(BF16)
    return high, (x - high.astype(F32)).astype(BF16)


def kernel(
    n,
    stages,
    total_rows,
    off_ref,
    tiles_hbm,
    start_hbm,
    gram_ref,
    final_ref,
    raw,
    first,
    fwd_high,
    fwd_low,
    adj_high,
    adj_low,
    basis,
    field,
    image,
    parts,
    acc,
    halo,
    give,
    got,
    scale,
    gacc,
    grow,
    box_a,
    box_b,
    box_c,
    totals,
    load_sem,
    acc_send,
    acc_recv,
    part_send,
    part_recv,
    sum_send,
    sum_recv,
):
    nblk, slots, tile, _ = raw.shape
    streams = basis.shape[0]
    width = basis.shape[3]
    probes = streams * width
    last_pair = OUTER * DEPTH - 1
    me = lax.axis_index("blk")
    slow = lax.rem(me, 2)
    fast = 1 - slow

    load_start = pltpu.make_async_copy(start_hbm, first, load_sem.at[0])
    load_start.start()
    load_tiles = pltpu.make_async_copy(tiles_hbm, raw, load_sem.at[1])
    load_tiles.start()

    barrier = pltpu.get_barrier_semaphore()

    def bit(b):
        return lax.rem(me // (1 << b), 2)

    def flipped(st, mask):
        other = me
        for m, b in enumerate(stages[st]):
            if mask >> m & 1:
                other = other + (1 << b) * (1 - 2 * bit(b))
        return other

    def masks(st):
        return range(1, 1 << len(stages[st]))

    others = [lax.rem(me + n - 1, n), lax.rem(me + 1, n)]
    others += [flipped(st, mask) for st in range(len(stages)) for mask in masks(st)]
    for other in others:
        pl.semaphore_signal(barrier, inc=1, device_id=(other,), device_id_type=MESH)

    def block(side, k):
        return side * (nblk - 1) + k * (1 - 2 * side)

    def beyond(side, k):
        return side * (nblk + 1 + 2 * k) - 1 - k

    def neighbour(side):
        return (lax.rem(me + n - 1 + 2 * side, n),)

    def acc_copy(slot, s, side, k, there):
        return pltpu.make_async_remote_copy(
            src_ref=acc.at[s, block(side, k)],
            dst_ref=halo.at[slot, s, there, k],
            send_sem=acc_send.at[slot, s, side, k],
            recv_sem=acc_recv.at[slot, s, there, k],
            device_id=neighbour(side),
            device_id_type=MESH,
        )

    def part_copy(slot, s, side, k, there):
        return pltpu.make_async_remote_copy(
            src_ref=give.at[s, side, k],
            dst_ref=got.at[slot, s, there, k],
            send_sem=part_send.at[slot, s, side, k],
            recv_sem=part_recv.at[slot, s, there, k],
            device_id=neighbour(side),
            device_id_type=MESH,
        )

    boxes = [box_a, box_b, box_c]

    def place(st):
        return sum(bit(b) << m for m, b in enumerate(stages[st]))

    def stage_copy(o, kind, st, mask):
        return pltpu.make_async_remote_copy(
            src_ref=boxes[kind].at[o, st, place(st)],
            dst_ref=boxes[kind].at[o, st, place(st)],
            send_sem=sum_send.at[o, kind, st, mask - 1],
            recv_sem=sum_recv.at[o, kind, st, mask - 1],
            device_id=(flipped(st, mask),),
            device_id_type=MESH,
        )

    def stage_open(o, kind, st, value):
        boxes[kind][o, st, place(st)] = value
        for mask in masks(st):
            stage_copy(o, kind, st, mask).start()

    def group_open(o, kind):
        begin, count = GROUPS[kind]
        stage_open(o, kind, 0, grow[o, pl.ds(begin, count)])

    def advance(o, kind, st):
        for mask in masks(st):
            stage_copy(o, kind, st, mask).wait()
        value = boxes[kind][o, st, 0]
        for m in masks(st):
            value = value + boxes[kind][o, st, m]
        if st + 1 < len(stages):
            stage_open(o, kind, st + 1, value)
        else:
            begin, count = GROUPS[kind]
            totals[o, pl.ds(begin, count)] = value

    lap = streams * DEPTH
    agenda = {}
    taken = {}
    for o, kind, whens in [
        (0, 0, [2 * streams]),
        (0, 1, [3 * streams, 4 * streams]),
        (0, 2, [5 * streams - 1, 5 * streams + 1]),
        (1, 0, [lap + 2 * streams, lap + 3 * streams]),
        (1, 1, [lap + 3 * streams, lap + 4 * streams - 1]),
        (1, 2, []),
    ]:
        for st, when in enumerate(whens[: len(stages)]):
            agenda.setdefault(when, []).append((o, kind, st))
        taken[o, kind] = min(len(whens), len(stages))

    def point(at):
        for when, steps in agenda.items():

            @pl.when(at == when)
            def _():
                for step in steps:
                    advance(*step)

    def finish(o, kind):
        for st in range(taken[o, kind], len(stages)):
            advance(o, kind, st)

    def ranks(i):
        offs = [off_ref[i, k] for k in range(slots)]
        return offs, [
            sum((offs[m] < offs[k]).astype(jnp.int32) for m in range(slots) if m != k)
            for k in range(slots)
        ]

    def sorted_slot(i, s):
        offs, rank = ranks(i)
        index, off = 0, 0
        for k in range(slots):
            index = jnp.where(rank[k] == s, k, index)
            off = jnp.where(rank[k] == s, offs[k], off)
        return index, off

    def source(i, d):
        offs, rank = ranks(i)
        index = nblk * slots
        for k in range(slots):
            index = jnp.where(offs[k] == d, i * slots + rank[k], index)
        return index

    def keep(ref, where, value):
        high, low = halves(value)
        ref[where + (pl.ds(0, width),)] = high
        ref[where + (pl.ds(width, width),)] = low

    def product(lhs, high, low):
        top = jnp.dot(lhs, high, preferred_element_type=F32)
        bottom = jnp.dot(lhs[:width], low, preferred_element_type=F32)
        return top[:width] + (top[width:] + bottom)

    def forward(s, i, begin, count):
        lhs = jnp.concatenate(
            [field[s, i + REACH + sorted_slot(i, begin + m)[1]] for m in range(count)], axis=1
        )
        span = pl.ds(pl.multiple_of(begin * tile, tile), count * tile)
        return product(lhs, fwd_high[i, span], fwd_low[i, span])

    def adjoint(s, i, begin, count):
        for m in range(count):
            k = begin + m
            parts[i * slots + k] = product(image[s, i], adj_high[i, k], adj_low[i, k])

    def edge(side, k):
        return side * (slots - REACH + k), REACH - k

    def inner(side, k):
        return (1 - side) * (REACH - k), slots - REACH + k

    middle = list(range(REACH, nblk - REACH))

    def rows_of(tl):
        return 1 + (tl + 1) // 2

    def first_row(tl):
        at = 0
        for t in range(1, SIZE):
            at = at + (FIRST[t] - FIRST[t - 1]) * (tl >= t)
        return at

    def gram_rows(o, tl, s):
        base = o * SIZE

        def one(v, carry):
            u = jnp.where(v == 0, tl, 2 * v - 1 - lax.rem(tl, 2))
            total = basis[s, base + tl, 0] * basis[s, base + u, 0]
            for i in range(1, nblk):
                total = total + basis[s, base + tl, i] * basis[s, base + u, i]
            lanes = total[:, :128]
            for c in range(128, tile, 128):
                lanes = lanes + total[:, c : c + 128]
            gacc[lax.rem(tl, 2), v, s] = lanes
            return carry

        lax.fori_loop(0, rows_of(tl), one, 0)

    def gram_close(o, tl):
        begin = first_row(tl)

        def one(v, carry):
            m = gacc[lax.rem(tl, 2), v].reshape(probes, 128).T
            grow[o, pl.ds(begin + v, 1), :] = jnp.sum(m, axis=0, keepdims=True)
            return carry

        lax.fori_loop(0, rows_of(tl), one, 0)
        for kind, last in enumerate(CLOSES):

            @pl.when(tl == last)
            def _():
                group_open(o, kind)

    def provisional(o):
        row = FIRST[GAUGE]
        return 1.0 / jnp.sqrt(totals[o, row : row + 1, :] / total_rows * GROWTH + 0.25)

    def gram(o, tl, s):
        gram_rows(o, tl, s)
        pl.when(s == streams - 1)(functools.partial(gram_close, o, tl))

    def phase(g, s):
        o, tl = g // DEPTH, 2 * lax.rem(g, DEPTH)
        t, slot = 2 * g, lax.rem(g, 2)
        which = ((tl == 0) & (g > 0)).astype(jnp.int32)

        @pl.when((s == 0) & (which == 1))
        def _():
            finish(0, 0)
            full = jnp.broadcast_to(provisional(0), (128, probes)).T
            for m in range(streams):
                for c in range(0, tile, 128):
                    scale[1, m, :, pl.ds(c, 128)] = full[m * width : (m + 1) * width]

        factor = scale[which, s]
        for i in middle:
            p = acc[s, i] * factor
            basis[s, t, i] = p
            keep(field, (s, i + REACH), p)
        for side in (fast, slow):
            for k in range(REACH):
                acc_copy(slot, s, side, k, side).wait()

                @pl.when(g > 0)
                def _():
                    part_copy(slot, s, side, k, side).wait()

                i = block(side, k)
                p = (acc[s, i] + got[slot, s, side, k]) * factor
                basis[s, t, i] = p
                keep(field, (s, i + REACH), p)
                beside = (halo[slot, s, side, k] + give[s, side, k]) * factor
                keep(field, (s, beyond(side, k) + REACH), beside)
            if side is fast:
                partial = [forward(s, block(fast, k), *edge(fast, k)) for k in range(REACH)]

        def image_row(i, q):
            basis[s, t + 1, i] = q
            keep(image, (s, i), q)

        def hand_over(side):
            for k in range(REACH):
                total = None
                for r in range(REACH - k):
                    term = parts[source(block(side, r), (2 * side - 1) * (r + 1 + k))]
                    total = term if total is None else total + term
                give[s, side, k] = total
                part_copy(1 - slot, s, side, k, 1 - side).start()

        for k in range(REACH):
            i = block(slow, k)
            image_row(i, forward(s, i, 0, slots))
        for k in range(REACH):
            i = block(fast, k)
            image_row(i, partial[k] + forward(s, i, *inner(fast, k)))
        for i in middle:
            image_row(i, forward(s, i, 0, slots))

        @pl.when(g == last_pair)
        def _():
            gram(o, tl, s)
            gram(o, tl + 1, s)

        for k in range(REACH):
            adjoint(s, block(slow, k), *edge(slow, k))
        hand_over(slow)
        for k in range(REACH):
            adjoint(s, block(slow, k), *inner(slow, k))
            adjoint(s, block(fast, k), 0, slots)
        for i in middle:
            adjoint(s, i, 0, slots)
        for i in range(nblk):
            total = None
            for r in range(nblk):
                if abs(i - r) <= REACH:
                    term = parts[source(r, i - r)]
                    total = term if total is None else total + term
            acc[s, i] = total

        @pl.when(g < last_pair)
        def _():
            for k in range(REACH):
                acc_copy(1 - slot, s, slow, k, 1 - slow).start()

        hand_over(fast)

        @pl.when(g < last_pair)
        def _():
            for k in range(REACH):
                acc_copy(1 - slot, s, fast, k, 1 - fast).start()
            gram(o, tl, s)
            gram(o, tl + 1, s)

        point(streams * g + s)

    grow[...] = jnp.zeros_like(grow)
    parts[nblk * slots] = jnp.zeros((width, tile), F32)
    scale[...] = jnp.ones_like(scale)
    give[...] = jnp.zeros_like(give)
    got[0] = jnp.zeros_like(got[0])
    load_start.wait()

    def turn(i):
        value = first[i].T
        for s in range(streams):
            acc[s, i] = value[s * width : (s + 1) * width]

    for k in range(REACH):
        turn(block(slow, k))
    pl.semaphore_wait(barrier, len(others))
    for s in range(streams):
        for k in range(REACH):
            acc_copy(0, s, slow, k, 1 - slow).start()
    for k in range(REACH):
        turn(block(fast, k))
    for s in range(streams):
        for k in range(REACH):
            acc_copy(0, s, fast, k, 1 - fast).start()
    for i in middle:
        turn(i)
    load_tiles.wait()

    def prepare(i, carry):
        for s in range(slots):
            value = raw[i, sorted_slot(i, s)[0]]
            high, low = halves(value)
            adj_high[i, s] = high
            adj_low[i, s] = low
            high, low = halves(value.T)
            fwd_high[i, pl.ds(s * tile, tile)] = high
            fwd_low[i, pl.ds(s * tile, tile)] = low
        return carry

    lax.fori_loop(0, nblk, prepare, 0)

    def pair(g, carry):
        def stream(s, c):
            phase(g, s)
            return c

        return lax.fori_loop(0, streams, stream, carry)

    lax.fori_loop(0, last_pair + 1, pair, 0)

    def last(s):
        slot = (last_pair + 1) % 2
        for side in (fast, slow):
            for k in range(REACH):
                i = block(side, k)
                part_copy(slot, s, side, k, side).wait()
                acc[s, i] += got[slot, s, side, k]

    for s in range(streams):
        last(s)

    for kind in range(len(GROUPS)):
        finish(OUTER - 1, kind)
    if OUTER > 1:
        for kind in range(1, len(GROUPS)):
            finish(0, kind)
    true = jnp.ones((1, probes), F32)
    for o in range(OUTER):
        for a in range(SIZE):
            for b in range(SIZE):
                x, y = a % DEPTH, b % DEPTH
                if a // DEPTH == b // DEPTH:
                    row = FIRST[x + y + a // DEPTH]
                else:
                    x, y = (x, y) if a < DEPTH else (y, x)
                    row = FIRST[2 * y + 1] + 1 + x if x <= y else FIRST[2 * x] + 1 + y
                value = totals[o, row : row + 1, :] / total_rows
                gram_ref[o, pl.ds(a * SIZE + b, 1), :] = value * true * true
        row = FIRST[SIZE - 1]
        corner = totals[o, row : row + 1, :] / total_rows * true * true
        norm = true / jnp.sqrt(corner + 0.25)
        if o < OUTER - 1:
            true = norm / provisional(o)
    for i in range(nblk):
        value = jnp.concatenate([acc[s, i] for s in range(streams)], axis=0)
        final_ref[i] = value.T * norm


def on_device(tiles, offsets, start):
    n = lax.axis_size("blk")
    levels = n.bit_length() - 1
    assert n == 1 << levels
    bits = [[0, 3, 4], [1, 2]] + [[b, b + 1] for b in range(5, levels, 2)]
    stages = [kept for group in bits if (kept := [b for b in group if b < levels])]
    nblk, slots, tile, _ = tiles.shape
    rows, probes = start.shape
    assert nblk >= 2 * REACH and slots >= REACH and OUTER == 2
    streams = STREAMS
    width = probes // streams
    dma = pltpu.SemaphoreType.DMA
    wide = (nblk, slots * tile, tile)
    square = (nblk, slots, tile, tile)
    grams, final = pl.pallas_call(
        functools.partial(kernel, n, stages, float(rows * n)),
        out_shape=(
            jax.ShapeDtypeStruct((OUTER, SIZE * SIZE, probes), F32),
            jax.ShapeDtypeStruct((nblk, tile, probes), F32),
        ),
        in_specs=[
            pl.BlockSpec(memory_space=pltpu.SMEM),
            pl.BlockSpec(memory_space=pl.ANY),
            pl.BlockSpec(memory_space=pl.ANY),
        ],
        out_specs=(pl.BlockSpec(memory_space=pltpu.VMEM), pl.BlockSpec(memory_space=pltpu.VMEM)),
        scratch_shapes=[
            pltpu.VMEM(tiles.shape, F32),
            pltpu.VMEM((nblk, tile, probes), F32),
            pltpu.VMEM(wide, BF16),
            pltpu.VMEM(wide, BF16),
            pltpu.VMEM(square, BF16),
            pltpu.VMEM(square, BF16),
            pltpu.VMEM((streams, OUTER * SIZE, nblk, width, tile), F32),
            pltpu.VMEM((streams, nblk + 2 * REACH, 2 * width, tile), BF16),
            pltpu.VMEM((streams, nblk, 2 * width, tile), BF16),
            pltpu.VMEM((nblk * slots + 1, width, tile), F32),
            pltpu.VMEM((streams, nblk, width, tile), F32),
            pltpu.VMEM((2, streams, 2, REACH, width, tile), F32),
            pltpu.VMEM((streams, 2, REACH, width, tile), F32),
            pltpu.VMEM((2, streams, 2, REACH, width, tile), F32),
            pltpu.VMEM((2, streams, width, tile), F32),
            pltpu.VMEM((2, 1 + DEPTH, streams, width, 128), F32),
            pltpu.VMEM((OUTER, 32, probes), F32),
        ]
        + [pltpu.VMEM((OUTER, len(stages), 8, count, probes), F32) for _, count in GROUPS]
        + [
            pltpu.VMEM((OUTER, 32, probes), F32),
            dma((2,)),
            dma((2, streams, 2, REACH)),
            dma((2, streams, 2, REACH)),
            dma((2, streams, 2, REACH)),
            dma((2, streams, 2, REACH)),
            dma((OUTER, len(GROUPS), len(stages), 7)),
            dma((OUTER, len(GROUPS), len(stages), 7)),
        ],
        compiler_params=pltpu.CompilerParams(collective_id=0, has_side_effects=True),
    )(offsets, tiles, start.reshape(nblk, tile, probes))
    return grams.reshape(OUTER, SIZE, SIZE, probes), final.reshape(rows, probes)


def solution(mesh):
    placed = (P("blk", None, None, None), P("blk", None), P("blk", None))
    return jax.shard_map(
        on_device, mesh=mesh, in_specs=placed, out_specs=(P(), P("blk", None)), check_vma=False
    )
```

time: 142 us -> 112 us (0.79)
  Pallas kernels: 138 us -> 108 us
    pallas_call x1, Pallas kernels: 138 us -> 108 us  [on_device(): pl.pallas_call(functools.partial(kernel, n, stages, float(rows * n)), out...]
where the time goes in v1:
time: 112 us
  Pallas kernels  108 us (96%)
  local copies, waits for them, and re-layouts  3.34 us (3%)
    pallas_call x1, Pallas kernels, on_device(): pl.pallas_call(functools.partial(kernel, n, stages, float(rows * n)), out...  108 us
    unnamed x2, local copies, waits for them, and re-layouts  3.34 us

profile of v1, /device:TPU:0, one launch (start us, length us, event | category | flops | bytes accessed | tf_op | source)
XLA Modules:
  0.0 112.0 jit_solution(10890391859744251067)
XLA Ops:
  0.6 108.0 %shard_map.50 = (f32[2,64,128]{2,1,0:T(8,128)}, f32[4,256,128]{2,1,0:T(8,128)}) custom-call(s32[4,3]{1,0:T(4,128)} %off_ref.1, f32[4,3,256,256]{3,2,1,0:T(8,128)} %tiles_hbm.1, f32[4,256,128]{2,1,0:T(8,128)} %bitcast.3), custom_call_target="tpu_custom_call" | custom-call | tf_op jit(solution)/shard_map/pallas_call | solution.py:489
  108.7 1.5 %copy.7 = f32[2,8,8,128]{3,2,1,0:T(8,128)} copy(f32[2,8,8,128]{3,2,1,0:T(8,128)} %bitcast.5) | data formatting | bytes 131072
  110.1 1.9 %copy.8 = f32[1024,128]{1,0:T(8,128)} copy(f32[1024,128]{1,0:T(8,128)} %bitcast.4) | data formatting | bytes 1048576

commit v2 on v1

--- a/solution.py
+++ b/solution.py
@@ -12,9 +12,9 @@
 DEPTH = 4
 SIZE = 2 * DEPTH
 STREAMS = 2
-FIRST = [0, 1, 3, 5, 8, 11, 16, 20]
-GROUPS = [(0, 8), (8, 8), (16, 16)]
-CLOSES = [3, 5, 7]
+FIRST = [0, 1, 3, 5, 8, 11, 15, 24]
+GROUPS = [(0, 8), (8, 16), (24, 8)]
+CLOSES = [3, 6, 7]
 GAUGE = 3
 GROWTH = 2.0 ** (14 * (SIZE - 1 - GAUGE))
 MESH = pl.DeviceIdType.MESH
@@ -27,15 +27,21 @@
     return high, (x - high.astype(F32)).astype(BF16)
 
 
+def provisional(totals, o, total_rows):
+    row = FIRST[GAUGE]
+    return 1.0 / jnp.sqrt(totals[o, row : row + 1, :] / total_rows * GROWTH + 0.25)
+
+
 def kernel(
     n,
     stages,
     total_rows,
-    off_ref,
+    off_hbm,
     tiles_hbm,
     start_hbm,
-    gram_ref,
-    final_ref,
+    totals,
+    ends,
+    off_ref,
     raw,
     first,
     fwd_high,
@@ -56,7 +62,6 @@
     box_a,
     box_b,
     box_c,
-    totals,
     load_sem,
     acc_send,
     acc_recv,
@@ -78,6 +83,8 @@
     load_start.start()
     load_tiles = pltpu.make_async_copy(tiles_hbm, raw, load_sem.at[1])
     load_tiles.start()
+    load_offs = pltpu.make_async_copy(off_hbm, off_ref, load_sem.at[2])
+    load_offs.start()
 
     barrier = pltpu.get_barrier_semaphore()
 
@@ -169,10 +176,10 @@
     taken = {}
     for o, kind, whens in [
         (0, 0, [2 * streams]),
-        (0, 1, [3 * streams, 4 * streams]),
-        (0, 2, [5 * streams - 1, 5 * streams + 1]),
+        (0, 1, [5 * streams - 1, 5 * streams + 1]),
+        (0, 2, [6 * streams - 1, 6 * streams + 1]),
         (1, 0, [lap + 2 * streams, lap + 3 * streams]),
-        (1, 1, [lap + 3 * streams, lap + 4 * streams - 1]),
+        (1, 1, []),
         (1, 2, []),
     ]:
         for st, when in enumerate(whens[: len(stages)]):
@@ -247,45 +254,50 @@
         return 1 + (tl + 1) // 2
 
     def first_row(tl):
+        if isinstance(tl, int):
+            return FIRST[tl]
         at = 0
         for t in range(1, SIZE):
-            at = at + (FIRST[t] - FIRST[t - 1]) * (tl >= t)
+            at = at + (FIRST[t] - FIRST[t - 1]) * jnp.int32(tl >= t)
         return at
+
+    def repeat(count, body):
+        if isinstance(count, int):
+            for v in range(count):
+                body(v, 0)
+        else:
+            lax.fori_loop(0, count, body, 0)
 
     def gram_rows(o, tl, s):
         base = o * SIZE
 
         def one(v, carry):
-            u = jnp.where(v == 0, tl, 2 * v - 1 - lax.rem(tl, 2))
+            if isinstance(tl, int):
+                u = tl if v == 0 else 2 * v - 1 - tl % 2
+            else:
+                u = jnp.where(v == 0, tl, 2 * v - 1 - lax.rem(tl, 2))
             total = basis[s, base + tl, 0] * basis[s, base + u, 0]
             for i in range(1, nblk):
                 total = total + basis[s, base + tl, i] * basis[s, base + u, i]
             lanes = total[:, :128]
             for c in range(128, tile, 128):
                 lanes = lanes + total[:, c : c + 128]
-            gacc[lax.rem(tl, 2), v, s] = lanes
+            gacc[tl % 2, v, s] = lanes
             return carry
 
-        lax.fori_loop(0, rows_of(tl), one, 0)
+        repeat(rows_of(tl), one)
 
     def gram_close(o, tl):
         begin = first_row(tl)
 
         def one(v, carry):
-            m = gacc[lax.rem(tl, 2), v].reshape(probes, 128).T
+            m = gacc[tl % 2, v].reshape(probes, 128).T
             grow[o, pl.ds(begin + v, 1), :] = jnp.sum(m, axis=0, keepdims=True)
             return carry
 
-        lax.fori_loop(0, rows_of(tl), one, 0)
+        repeat(rows_of(tl), one)
         for kind, last in enumerate(CLOSES):
-
-            @pl.when(tl == last)
-            def _():
-                group_open(o, kind)
-
-    def provisional(o):
-        row = FIRST[GAUGE]
-        return 1.0 / jnp.sqrt(totals[o, row : row + 1, :] / total_rows * GROWTH + 0.25)
+            pl.when(tl == last)(functools.partial(group_open, o, kind))
 
     def gram(o, tl, s):
         gram_rows(o, tl, s)
@@ -299,7 +311,7 @@
         @pl.when((s == 0) & (which == 1))
         def _():
             finish(0, 0)
-            full = jnp.broadcast_to(provisional(0), (128, probes)).T
+            full = jnp.broadcast_to(provisional(totals, 0, total_rows), (128, probes)).T
             for m in range(streams):
                 for c in range(0, tile, 128):
                     scale[1, m, :, pl.ds(c, 128)] = full[m * width : (m + 1) * width]
@@ -350,8 +362,7 @@
 
         @pl.when(g == last_pair)
         def _():
-            gram(o, tl, s)
-            gram(o, tl + 1, s)
+            gram(OUTER - 1, SIZE - 1, s)
 
         for k in range(REACH):
             adjoint(s, block(slow, k), *edge(slow, k))
@@ -383,6 +394,10 @@
             gram(o, tl, s)
             gram(o, tl + 1, s)
 
+        @pl.when(g == last_pair)
+        def _():
+            gram(OUTER - 1, SIZE - 2, s)
+
         point(streams * g + s)
 
     grow[...] = jnp.zeros_like(grow)
@@ -411,6 +426,7 @@
     for i in middle:
         turn(i)
     load_tiles.wait()
+    load_offs.wait()
 
     def prepare(i, carry):
         for s in range(slots):
@@ -440,17 +456,26 @@
             for k in range(REACH):
                 i = block(side, k)
                 part_copy(slot, s, side, k, side).wait()
-                acc[s, i] += got[slot, s, side, k]
-
-    for s in range(streams):
+                ends[s, i] = acc[s, i] + got[slot, s, side, k]
+        for i in middle:
+            ends[s, i] = acc[s, i]
+
+    for s in range(streams - 1):
         last(s)
-
-    for kind in range(len(GROUPS)):
+    advance(OUTER - 1, 2, 0)
+    advance(OUTER - 1, 1, 0)
+    last(streams - 1)
+    for kind in (2, 1, 0):
+        taken[OUTER - 1, kind] = max(taken[OUTER - 1, kind], 1)
         finish(OUTER - 1, kind)
     if OUTER > 1:
         for kind in range(1, len(GROUPS)):
             finish(0, kind)
-    true = jnp.ones((1, probes), F32)
+
+
+def closing(total_rows, totals, ends, gram_ref, final_ref):
+    streams, nblk, _, _ = ends.shape
+    true = jnp.ones((1, totals.shape[2]), F32)
     for o in range(OUTER):
         for a in range(SIZE):
             for b in range(SIZE):
@@ -466,9 +491,9 @@
         corner = totals[o, row : row + 1, :] / total_rows * true * true
         norm = true / jnp.sqrt(corner + 0.25)
         if o < OUTER - 1:
-            true = norm / provisional(o)
+            true = norm / provisional(totals, o, total_rows)
     for i in range(nblk):
-        value = jnp.concatenate([acc[s, i] for s in range(streams)], axis=0)
+        value = jnp.concatenate([ends[s, i] for s in range(streams)], axis=0)
         final_ref[i] = value.T * norm
 
 
@@ -486,19 +511,22 @@
     dma = pltpu.SemaphoreType.DMA
     wide = (nblk, slots * tile, tile)
     square = (nblk, slots, tile, tile)
-    grams, final = pl.pallas_call(
+    whole = pl.BlockSpec(memory_space=pltpu.VMEM)
+    operands = (offsets, tiles, start.reshape(nblk, tile, probes))
+    totals, ends = pl.pallas_call(
         functools.partial(kernel, n, stages, float(rows * n)),
         out_shape=(
-            jax.ShapeDtypeStruct((OUTER, SIZE * SIZE, probes), F32),
-            jax.ShapeDtypeStruct((nblk, tile, probes), F32),
+            pltpu.VMEM((OUTER, 32, probes), F32),
+            pltpu.VMEM((streams, nblk, width, tile), F32),
         ),
         in_specs=[
-            pl.BlockSpec(memory_space=pltpu.SMEM),
+            pl.BlockSpec(memory_space=pl.ANY),
             pl.BlockSpec(memory_space=pl.ANY),
             pl.BlockSpec(memory_space=pl.ANY),
         ],
-        out_specs=(pl.BlockSpec(memory_space=pltpu.VMEM), pl.BlockSpec(memory_space=pltpu.VMEM)),
+        out_specs=(whole, whole),
         scratch_shapes=[
+            pltpu.SMEM(offsets.shape, jnp.int32),
             pltpu.VMEM(tiles.shape, F32),
             pltpu.VMEM((nblk, tile, probes), F32),
             pltpu.VMEM(wide, BF16),
@@ -519,8 +547,7 @@
         ]
         + [pltpu.VMEM((OUTER, len(stages), 8, count, probes), F32) for _, count in GROUPS]
         + [
-            pltpu.VMEM((OUTER, 32, probes), F32),
-            dma((2,)),
+            dma((3,)),
             dma((2, streams, 2, REACH)),
             dma((2, streams, 2, REACH)),
             dma((2, streams, 2, REACH)),
@@ -528,8 +555,20 @@
             dma((OUTER, len(GROUPS), len(stages), 7)),
             dma((OUTER, len(GROUPS), len(stages), 7)),
         ],
-        compiler_params=pltpu.CompilerParams(collective_id=0, has_side_effects=True),
-    )(offsets, tiles, start.reshape(nblk, tile, probes))
+        compiler_params=pltpu.CompilerParams(
+            collective_id=0, has_side_effects=True, vmem_limit_bytes=48 << 20
+        ),
+    )(*[pltpu.with_memory_space_constraint(x, pltpu.HBM) for x in operands])
+    grams, final = pl.pallas_call(
+        functools.partial(closing, float(rows * n)),
+        out_shape=(
+            jax.ShapeDtypeStruct((OUTER, SIZE * SIZE, probes), F32),
+            jax.ShapeDtypeStruct((nblk, tile, probes), F32),
+        ),
+        in_specs=[whole, whole],
+        out_specs=(whole, whole),
+        compiler_params=pltpu.CompilerParams(vmem_limit_bytes=8 << 20),
+    )(totals, ends)
     return grams.reshape(OUTER, SIZE, SIZE, probes), final.reshape(rows, probes)
 
 

time: 112 us -> 108 us (0.964)
  local copies, waits for them, and re-layouts: 3.34 us -> 0 us
    unnamed x2 -> x0, local copies, waits for them, and re-layouts: 3.34 us -> none
    pallas_call x1, Pallas kernels: 108 us -> 106 us  [on_device(): pl.pallas_call(functools.partial(kernel, n, stages, float(rows * n)), out...]
where the time goes in v2:
time: 108 us
  Pallas kernels  107 us (99%)
    pallas_call x1, Pallas kernels, on_device(): pl.pallas_call(functools.partial(kernel, n, stages, float(rows * n)), out...  106 us

profile of v2, /device:TPU:0, one launch (start us, length us, event | category | flops | bytes accessed | tf_op | source)
XLA Modules:
  0.0 108.0 jit_solution(7715467719704334220)
XLA Ops:
  0.6 106.3 %shard_map.50 = (f32[2,32,128]{2,1,0:T(8,128)S(1)}, f32[2,4,64,256]{3,2,1,0:T(8,128)S(1)}) custom-call(s32[4,3]{1,0:T(4,128)} %off_hbm.1, f32[4,3,256,256]{3,2,1,0:T(8,128)} %tiles_hbm.1, f32[4,256,128]{2,1,0:T(8,128)} %bitcast.3), custom_call_target="tpu_custom_call" | custom-call | tf_op jit(solution)/shard_map/pallas_call | solution.py:516
  107.0 1.0 shard_map.51

commit v3 on v2

--- a/solution.py
+++ b/solution.py
@@ -62,6 +62,7 @@
     box_a,
     box_b,
     box_c,
+    start_sem,
     load_sem,
     acc_send,
     acc_recv,
@@ -79,11 +80,24 @@
     slow = lax.rem(me, 2)
     fast = 1 - slow
 
-    load_start = pltpu.make_async_copy(start_hbm, first, load_sem.at[0])
-    load_start.start()
-    load_tiles = pltpu.make_async_copy(tiles_hbm, raw, load_sem.at[1])
+    def load_start(i):
+        return pltpu.make_async_copy(start_hbm.at[i], first.at[i], start_sem.at[i])
+
+    load_tiles = pltpu.make_async_copy(tiles_hbm, raw, load_sem.at[0])
+    load_offs = pltpu.make_async_copy(off_hbm, off_ref, load_sem.at[1])
+
+    def block(side, k):
+        return side * (nblk - 1) + k * (1 - 2 * side)
+
+    def beyond(side, k):
+        return side * (nblk + 1 + 2 * k) - 1 - k
+
+    for side in (slow, fast):
+        for k in range(REACH):
+            load_start(block(side, k)).start()
+    for i in range(REACH, nblk - REACH):
+        load_start(i).start()
     load_tiles.start()
-    load_offs = pltpu.make_async_copy(off_hbm, off_ref, load_sem.at[2])
     load_offs.start()
 
     barrier = pltpu.get_barrier_semaphore()
@@ -105,12 +119,6 @@
     others += [flipped(st, mask) for st in range(len(stages)) for mask in masks(st)]
     for other in others:
         pl.semaphore_signal(barrier, inc=1, device_id=(other,), device_id_type=MESH)
-
-    def block(side, k):
-        return side * (nblk - 1) + k * (1 - 2 * side)
-
-    def beyond(side, k):
-        return side * (nblk + 1 + 2 * k) - 1 - k
 
     def neighbour(side):
         return (lax.rem(me + n - 1 + 2 * side, n),)
@@ -338,6 +346,10 @@
             if side is fast:
                 partial = [forward(s, block(fast, k), *edge(fast, k)) for k in range(REACH)]
 
+        @pl.when(g == last_pair)
+        def _():
+            gram(OUTER - 1, SIZE - 2, s)
+
         def image_row(i, q):
             basis[s, t + 1, i] = q
             keep(image, (s, i), q)
@@ -394,10 +406,6 @@
             gram(o, tl, s)
             gram(o, tl + 1, s)
 
-        @pl.when(g == last_pair)
-        def _():
-            gram(OUTER - 1, SIZE - 2, s)
-
         point(streams * g + s)
 
     grow[...] = jnp.zeros_like(grow)
@@ -405,9 +413,9 @@
     scale[...] = jnp.ones_like(scale)
     give[...] = jnp.zeros_like(give)
     got[0] = jnp.zeros_like(got[0])
-    load_start.wait()
 
     def turn(i):
+        load_start(i).wait()
         value = first[i].T
         for s in range(streams):
             acc[s, i] = value[s * width : (s + 1) * width]
@@ -462,10 +470,10 @@
 
     for s in range(streams - 1):
         last(s)
+    advance(OUTER - 1, 1, 0)
     advance(OUTER - 1, 2, 0)
-    advance(OUTER - 1, 1, 0)
     last(streams - 1)
-    for kind in (2, 1, 0):
+    for kind in (1, 2, 0):
         taken[OUTER - 1, kind] = max(taken[OUTER - 1, kind], 1)
         finish(OUTER - 1, kind)
     if OUTER > 1:
@@ -547,7 +555,8 @@
         ]
         + [pltpu.VMEM((OUTER, len(stages), 8, count, probes), F32) for _, count in GROUPS]
         + [
-            dma((3,)),
+            dma((nblk,)),
+            dma((2,)),
             dma((2, streams, 2, REACH)),
             dma((2, streams, 2, REACH)),
             dma((2, streams, 2, REACH)),

time: 108 us -> 107 us (level)
    pallas_call x1, Pallas kernels: 106 us -> 105 us  [on_device(): pl.pallas_call(functools.partial(kernel, n, stages, float(rows * n)), out...]
where the time goes in v3:
time: 107 us
  Pallas kernels  106 us (99%)
    pallas_call x1, Pallas kernels, on_device(): pl.pallas_call(functools.partial(kernel, n, stages, float(rows * n)), out...  105 us

profile of v3, /device:TPU:0, one launch (start us, length us, event | category | flops | bytes accessed | tf_op | source)
XLA Modules:
  0.0 106.6 jit_solution(13260283098791213769)
XLA Ops:
  0.6 105.0 %shard_map.50 = (f32[2,32,128]{2,1,0:T(8,128)S(1)}, f32[2,4,64,256]{3,2,1,0:T(8,128)S(1)}) custom-call(s32[4,3]{1,0:T(4,128)} %off_hbm.1, f32[4,3,256,256]{3,2,1,0:T(8,128)} %tiles_hbm.1, f32[4,256,128]{2,1,0:T(8,128)} %bitcast.3), custom_call_target="tpu_custom_call" | custom-call | tf_op jit(solution)/shard_map/pallas_call | solution.py:524
  105.6 1.0 shard_map.51

commit v4 on v3

--- a/solution.py
+++ b/solution.py
@@ -12,9 +12,9 @@
 DEPTH = 4
 SIZE = 2 * DEPTH
 STREAMS = 2
-FIRST = [0, 1, 3, 5, 8, 11, 15, 24]
-GROUPS = [(0, 8), (8, 16), (24, 8)]
-CLOSES = [3, 6, 7]
+FIRST = [0, 1, 3, 5, 8, 11, 16, 24]
+GROUPS = [(0, 8), (8, 8), (16, 8), (24, 8)]
+CLOSES = [3, 5, 6, 7]
 GAUGE = 3
 GROWTH = 2.0 ** (14 * (SIZE - 1 - GAUGE))
 MESH = pl.DeviceIdType.MESH
@@ -62,6 +62,7 @@
     box_a,
     box_b,
     box_c,
+    box_d,
     start_sem,
     load_sem,
     acc_send,
@@ -143,7 +144,7 @@
             device_id_type=MESH,
         )
 
-    boxes = [box_a, box_b, box_c]
+    boxes = [box_a, box_b, box_c, box_d]
 
     def place(st):
         return sum(bit(b) << m for m, b in enumerate(stages[st]))
@@ -184,11 +185,13 @@
     taken = {}
     for o, kind, whens in [
         (0, 0, [2 * streams]),
-        (0, 1, [5 * streams - 1, 5 * streams + 1]),
-        (0, 2, [6 * streams - 1, 6 * streams + 1]),
+        (0, 1, [4 * streams - 1, 5 * streams - 1]),
+        (0, 2, [5 * streams, 6 * streams]),
+        (0, 3, [6 * streams - 1, 7 * streams - 1]),
         (1, 0, [lap + 2 * streams, lap + 3 * streams]),
-        (1, 1, []),
+        (1, 1, [lap + 3 * streams, lap + 4 * streams - 1]),
         (1, 2, []),
+        (1, 3, []),
     ]:
         for st, when in enumerate(whens[: len(stages)]):
             agenda.setdefault(when, []).append((o, kind, st))
@@ -384,25 +387,30 @@
             adjoint(s, block(fast, k), 0, slots)
         for i in middle:
             adjoint(s, i, 0, slots)
-        for i in range(nblk):
+        def own_part(i):
             total = None
             for r in range(nblk):
-                if abs(i - r) <= REACH:
-                    term = parts[source(r, i - r)]
-                    total = term if total is None else total + term
+                term = parts[source(r, i - r)]
+                total = term if total is None else total + term
             acc[s, i] = total
+
+        def own_parts(side):
+            for k in range(REACH):
+                own_part(block(side, k))
+
+            @pl.when(g < last_pair)
+            def _():
+                for k in range(REACH):
+                    acc_copy(1 - slot, s, side, k, 1 - side).start()
+
+        own_parts(slow)
+        hand_over(fast)
+        own_parts(fast)
+        for i in middle:
+            own_part(i)
 
         @pl.when(g < last_pair)
         def _():
-            for k in range(REACH):
-                acc_copy(1 - slot, s, slow, k, 1 - slow).start()
-
-        hand_over(fast)
-
-        @pl.when(g < last_pair)
-        def _():
-            for k in range(REACH):
-                acc_copy(1 - slot, s, fast, k, 1 - fast).start()
             gram(o, tl, s)
             gram(o, tl + 1, s)
 
@@ -470,10 +478,10 @@
 
     for s in range(streams - 1):
         last(s)
-    advance(OUTER - 1, 1, 0)
     advance(OUTER - 1, 2, 0)
+    advance(OUTER - 1, 3, 0)
     last(streams - 1)
-    for kind in (1, 2, 0):
+    for kind in (2, 3, 1, 0):
         taken[OUTER - 1, kind] = max(taken[OUTER - 1, kind], 1)
         finish(OUTER - 1, kind)
     if OUTER > 1:

time: 107 us -> 107 us (level)
  no operation moved by 1% of the time
where the time goes in v4:
time: 107 us
  Pallas kernels  106 us (99%)
    pallas_call x1, Pallas kernels, on_device(): pl.pallas_call(functools.partial(kernel, n, stages, float(rows * n)), out...  105 us

profile of v4, /device:TPU:0, one launch (start us, length us, event | category | flops | bytes accessed | tf_op | source)
XLA Modules:
  0.0 106.6 jit_solution(12717937706494619532)
XLA Ops:
  0.6 104.9 %shard_map.50 = (f32[2,32,128]{2,1,0:T(8,128)S(1)}, f32[2,4,64,256]{3,2,1,0:T(8,128)S(1)}) custom-call(s32[4,3]{1,0:T(4,128)} %off_hbm.1, f32[4,3,256,256]{3,2,1,0:T(8,128)} %tiles_hbm.1, f32[4,256,128]{2,1,0:T(8,128)} %bitcast.3), custom_call_target="tpu_custom_call" | custom-call | tf_op jit(solution)/shard_map/pallas_call | solution.py:532
  105.6 1.0 shard_map.51
